TPU v7x, 32 devices: a whole 2x2x4 slice. The times are simulated.
32 devices in a mesh: grp: 2 (over x), tok: 8 (over z, y), mdl: 2 (over core).
Axes of the slice: x: 2, y: 2, z: 4, core: 2. Of those that a mesh axis runs over, the one named last changes fastest.
Arguments:
- hidden: bfloat16 [1024, 4096], P(('grp', 'tok'), 'mdl'), parts along dimension 0, may hold values from -3 to 3
- queries: bfloat16 [1024, 16, 128], P(('grp', 'tok'), 'mdl'), parts along dimension 0, may hold values from -8 to 8
- cache: bfloat16 [16, 2048, 4, 2, 128], P(('grp', 'tok'), None, 'mdl'), parts along dimension 0, may hold values from -8 to 8
- cache_lengths: int32 [16], P(('grp', 'tok')), parts along dimension 0, may hold values from 128 to 2048, as said below
- wkv: bfloat16 [4096, 4, 2, 128], P('tok', 'mdl'), may hold values from -0.09375 to 0.09375
- wo: bfloat16 [16, 128, 4096], P('mdl', None, 'tok'), may hold values from -0.5 to 0.5
- attn_gain: bfloat16 [4096], replicated, may hold values from 0.5 to 1.5
- moe_gain: bfloat16 [4096], replicated, may hold values from 0.5 to 1.5
- w_gate: bfloat16 [16, 4096, 1792], P(('tok', 'mdl')), may hold values from -0.09375 to 0.09375
- w_up: bfloat16 [16, 4096, 1792], P(('tok', 'mdl')), may hold values from -0.09375 to 0.09375
- w_down: bfloat16 [16, 1792, 4096], P(('tok', 'mdl')), may hold values from -0.0625 to 0.0625
- expert_ids: int32 [1024, 2], P(('grp', 'tok', 'mdl')), parts along dimension 0, may hold values from 0 to 3, all different within a row; in each aligned block of 32 rows (0 to 31, 32 to 63, ...) at most 18 rows name the same one
- gates: float32 [1024, 2], P(('grp', 'tok', 'mdl')), parts along dimension 0, may hold values from 0.1 to 1
Outputs:
- mixed: bfloat16 [1024, 4096], P(('grp', 'tok', 'mdl')), parts along dimension 0
- fresh_key_value: bfloat16 [1024, 4, 2, 128], P(('grp', 'tok'), 'mdl'), parts along dimension 0
There are 2 independent parts, one for each index of `grp`. A program takes and returns all parts, laid end to end along the dimension named above; an argument that names none is the same for every part. Nothing has to cross between parts.
Inputs may be any that keep to these rules, and one draw needn't show every extreme that they name: `expert_ids`: each token names 2 different experts; in aligned blocks of 32 rows no expert is named by more than 18 rows, a bound that some block reaches. `cache_lengths`: some rollout holds exactly 2048 cached positions.
All inputs are finite; a program needn't handle non-finite values.
Results may differ from a plain program's by a relative error of at most 0.007.
Values may be sent and summed in bfloat16 or wider, within the bound.
A program may use at most 128 MiB of HBM per device.

v0:
```python
import math

import jax
import jax.numpy as jnp
from jax import lax
from jax.sharding import PartitionSpec as P

EXPERTS = 4
TOPK = 2


eps_norm = 1e-05
rope_base = 1000000.0
mask_fill = -1e30


def rms_scale(values_in, gain):
    values = values_in.astype(jnp.float32)
    meansq = jnp.mean(values * values, axis=-1, keepdims=True)
    return values * lax.rsqrt(meansq + eps_norm) * gain.astype(jnp.float32)


def rotate(key_rows, positions):
    half_dim = key_rows.shape[-1] // 2
    inverse = jnp.exp(
        jnp.arange(half_dim, dtype=jnp.float32) * (-2.0 * math.log(rope_base) / key_rows.shape[-1])
    )
    angle = positions.astype(jnp.float32)[:, None] * inverse[None, :]
    cosine = jnp.cos(angle)[:, None, :]
    sine_vals = jnp.sin(angle)[:, None, :]
    front_half = key_rows[..., :half_dim]
    back_half = key_rows[..., half_dim:]
    return jnp.concatenate(
        [front_half * cosine - back_half * sine_vals, back_half * cosine + front_half * sine_vals],
        axis=-1,
    )


def score_rows(query_rows, key_rows, scale_factor):
    return (
        lax.dot_general(
            query_rows, key_rows, (((1,), (1,)), ((), ())), preferred_element_type=jnp.float32
        )
        * scale_factor
    )


def head_attention(query_rows, cache_keys, cache_values, length, new_keys, new_values, head_group):
    row_count = query_rows.shape[0]
    block_len = min(512, cache_keys.shape[0])
    scale_factor = 1.0 / math.sqrt(query_rows.shape[1])
    token_of_row = jnp.arange(row_count) // head_group
    block_total = (length + block_len - 1) // block_len

    def block_scores(block_idx):
        row_offset = block_idx * block_len
        block_keys = lax.dynamic_slice_in_dim(cache_keys, row_offset, block_len, 0)
        allowed = row_offset + jnp.arange(block_len) < length
        return (
            jnp.where(
                allowed[None, :], score_rows(query_rows, block_keys, scale_factor), mask_fill
            ),
            allowed,
        )

    new_allowed = jnp.arange(new_keys.shape[0])[None, :] <= token_of_row[:, None]
    new_scores = jnp.where(new_allowed, score_rows(query_rows, new_keys, scale_factor), mask_fill)
    first_max = jnp.max(new_scores, axis=1)
    first_sum = jnp.sum(
        jnp.where(new_allowed, jnp.exp(new_scores - first_max[:, None]), 0.0), axis=1
    )

    def first_pass(block_idx, carry):
        run_max, run_sum = carry
        scores, allowed = block_scores(block_idx)
        next_max = jnp.maximum(run_max, jnp.max(scores, axis=1))
        weights = jnp.where(allowed[None, :], jnp.exp(scores - next_max[:, None]), 0.0)
        return (next_max, run_sum * jnp.exp(run_max - next_max) + jnp.sum(weights, axis=1))

    row_max, row_sum = lax.fori_loop(0, block_total, first_pass, (first_max, first_sum))
    new_probs = (
        jnp.where(new_allowed, jnp.exp(new_scores - row_max[:, None]), 0.0) / row_sum[:, None]
    ).astype(jnp.bfloat16)
    start_total = jnp.dot(new_probs, new_values, preferred_element_type=jnp.float32)

    def second_pass(block_idx, total):
        scores, allowed = block_scores(block_idx)
        probs = (
            jnp.where(allowed[None, :], jnp.exp(scores - row_max[:, None]), 0.0) / row_sum[:, None]
        ).astype(jnp.bfloat16)
        block_values = lax.dynamic_slice_in_dim(cache_values, block_idx * block_len, block_len, 0)
        return total + jnp.dot(probs, block_values, preferred_element_type=jnp.float32)

    total = lax.fori_loop(0, block_total, second_pass, start_total)
    return total.astype(jnp.bfloat16)


def shards(
    hidden,
    queries,
    cache,
    cache_lengths,
    wkv,
    wo,
    attn_gain,
    moe_gain,
    w_gate,
    w_up,
    w_down,
    expert_ids,
    gates,
):
    full_rows = lax.all_gather(hidden, "mdl", axis=1, tiled=True)
    span_len = full_rows.shape[0]
    normalized_input = rms_scale(full_rows, attn_gain).astype(jnp.bfloat16)
    kv_heads = wkv.shape[1]
    head_dim = wkv.shape[3]
    weight_piece = lax.all_gather(wkv, "tok", axis=0, tiled=True)
    key_value_projection = jnp.dot(
        normalized_input,
        weight_piece.reshape(weight_piece.shape[0], -1),
        preferred_element_type=jnp.float32,
    ).reshape(span_len, kv_heads, 2, head_dim)
    length = cache_lengths[0]
    positions = length + jnp.arange(span_len, dtype=jnp.int32)
    fresh_key_value = jnp.stack(
        [rotate(key_value_projection[:, :, 0], positions), key_value_projection[:, :, 1]], axis=2
    ).astype(jnp.bfloat16)
    head_group = queries.shape[1] // kv_heads
    outputs = []
    for head_index in range(kv_heads):
        query_rows = queries[:, head_index * head_group : (head_index + 1) * head_group].reshape(
            span_len * head_group, head_dim
        )
        attended = head_attention(
            query_rows,
            cache[0, :, head_index, 0],
            cache[0, :, head_index, 1],
            length,
            fresh_key_value[:, head_index, 0],
            fresh_key_value[:, head_index, 1],
            head_group,
        )
        outputs.append(attended.reshape(span_len, head_group * head_dim))
    heads_out = jnp.concatenate(outputs, axis=1)
    weight_piece = lax.all_gather(wo, "tok", axis=2, tiled=True)
    attn_out = jnp.dot(
        heads_out,
        weight_piece.reshape(-1, weight_piece.shape[2]),
        preferred_element_type=jnp.float32,
    )
    core_rows = span_len // lax.axis_size("mdl")
    core_start = lax.axis_index("mdl") * core_rows
    summed_heads = lax.psum(attn_out, "mdl")
    attn_rows = lax.dynamic_slice_in_dim(summed_heads, core_start, core_rows, 0)
    resid = (
        lax.dynamic_slice_in_dim(full_rows, core_start, core_rows, 0).astype(jnp.float32)
        + attn_rows
    )
    moe_in = rms_scale(resid, moe_gain).astype(jnp.bfloat16)
    expert_range = jnp.arange(EXPERTS)
    matches = expert_ids[:, :, None] == expert_range[None, None, :]
    chosen = jnp.sum(matches.astype(jnp.int32), axis=1)
    route = jnp.sum(jnp.where(matches, gates[:, :, None], 0.0), axis=1)
    slot_of = jnp.cumsum(chosen, axis=0) - chosen
    capacity = core_rows * TOPK * 9 // (8 * EXPERTS)
    slot_range = jnp.arange(capacity)
    select = (slot_of.T[:, None, :] == slot_range[None, :, None]) & (chosen.T[:, None, :] > 0)
    send_rows = jnp.einsum(
        "eci,id->ecd", select.astype(jnp.bfloat16), moe_in, preferred_element_type=jnp.float32
    ).astype(jnp.bfloat16)
    owners = lax.axis_size("tok") * lax.axis_size("mdl")
    slabs = owners // EXPERTS
    model_width = moe_in.shape[1]
    core_count = lax.axis_size("mdl")
    send_chip = jnp.repeat(send_rows, slabs // core_count, axis=0)
    received = lax.all_to_all(send_chip, "tok", split_axis=0, concat_axis=0, tiled=True)
    chip_count = received.shape[0]
    item_count = received.shape[1]
    both_cores = lax.all_gather(received[:, None], "mdl", axis=1, tiled=True)
    received = both_cores.reshape(-1, item_count, model_width)
    flat_rows = received.reshape(-1, model_width)
    gate_val = jnp.dot(flat_rows, w_gate[0], preferred_element_type=jnp.float32)
    up_val = jnp.dot(flat_rows, w_up[0], preferred_element_type=jnp.float32)
    slab_hidden = (jax.nn.silu(gate_val) * up_val).astype(jnp.bfloat16)
    slab_out = jnp.dot(slab_hidden, w_down[0], preferred_element_type=jnp.float32).astype(
        jnp.bfloat16
    )
    slab_out = slab_out.reshape(received.shape)
    per_core = slab_out.reshape(chip_count, core_count, item_count, model_width).astype(jnp.float32)
    chip_total = lax.psum_scatter(
        per_core.astype(jnp.bfloat16), "mdl", scatter_dimension=1, tiled=True
    ).astype(jnp.float32)
    returned = lax.all_to_all(
        chip_total[:, 0].astype(jnp.bfloat16), "tok", split_axis=0, concat_axis=0, tiled=True
    ).astype(jnp.float32)
    summed = jnp.sum(returned.reshape(EXPERTS, slabs // core_count, capacity, model_width), axis=1)
    weight_table = select.astype(jnp.float32) * route.T[:, None, :]
    moe_out = jnp.einsum("eci,ecd->id", weight_table, summed, precision=lax.Precision.HIGHEST)
    mixed = (resid + moe_out).astype(jnp.bfloat16)
    return (mixed, fresh_key_value)


def solution(mesh):
    in_specs = (
        P(("grp", "tok"), "mdl"),
        P(("grp", "tok"), "mdl", None),
        P(("grp", "tok"), None, "mdl", None, None),
        P(("grp", "tok")),
        P("tok", "mdl", None, None),
        P("mdl", None, "tok"),
        P(),
        P(),
        P(("tok", "mdl"), None, None),
        P(("tok", "mdl"), None, None),
        P(("tok", "mdl"), None, None),
        P(("grp", "tok", "mdl"), None),
        P(("grp", "tok", "mdl"), None),
    )
    out_specs = (P(("grp", "tok", "mdl"), None), P(("grp", "tok"), "mdl", None, None))
    return jax.shard_map(shards, mesh=mesh, in_specs=in_specs, out_specs=out_specs, check_vma=False)
```

profile of v0, /device:TPU:0, one launch (start us, length us, event | category | flops | bytes accessed | tf_op | source)
XLA Modules:
  0.0 394.5 jit_solution(5354055071857114779)
XLA Ops:
  7.2 0.7 all-gather.5.cloned.1.call-update
  8.0 0.7 all-gather.7.cloned.1.call-update
  9.4 0.7 convert_element_type.71
  10.1 2.5 all_gather.12
  13.1 3.0 fusion.115
  16.4 69.3 %all-gather.5.cloned.1.call-done = bf16[4096,2,2,128]{3,2,1,0:T(2,128)(2,1)} async-done(((bf16[512,2,2,128]{3,2,1,0:T(2,128)(2,1)}), bf16[4096,2,2,128]{3,2,1,0:T(2,128)(2,1)}) %all-gather.5.cloned.1.call-update) | async-done | bytes 4194320 | tf_op jit(solution)/shard_map/all_gather | solution.py:118
  85.7 11.3 %copy.85 = bf16[4096,2,2,128]{0,3,2,1:T(8,128)(2,1)} copy(bf16[4096,2,2,128]{3,2,1,0:T(2,128)(2,1)} %all-gather.5.cloned.1.call-done) | data formatting | bytes 8388608 | tf_op jit(solution)/shard_map/reshape | solution.py:121
  97.0 3.7 fusion.119
  101.2 2.3 while.44
  101.3 0.7 add_compare_fusion.8
  102.4 0.7 add_compare_fusion.8
  103.7 2.5 while.45
  103.8 0.7 add_compare_fusion.9
  104.4 0.5 fusion.148
  105.0 0.7 add_compare_fusion.9
  105.6 0.5 fusion.148
  106.3 2.3 while.46
  106.3 0.7 add_compare_fusion.10
  107.0 0.3 fusion.150
  107.5 0.7 add_compare_fusion.10
  108.1 0.3 fusion.150
  108.8 2.5 while.47
  108.8 0.7 add_compare_fusion.11
  109.5 0.5 fusion.154
  110.0 0.7 add_compare_fusion.11
  110.7 0.5 fusion.154
  111.3 99.9 %all-gather.7.cloned.1.call-done = bf16[8,128,4096]{2,1,0:T(8,128)(2,1)} async-done(((bf16[8,128,512]{2,1,0:T(8,128)(2,1)}), bf16[8,128,4096]{2,1,0:T(8,128)(2,1)}) %all-gather.7.cloned.1.call-update) | async-done | bytes 8388624 | tf_op jit(solution)/shard_map/all_gather | solution.py:146
  211.2 6.1 %fusion.84 = f32[64,4096]{1,0:T(8,128)} fusion(bf16[1024,4096]{1,0:T(8,128)(2,1)} %bitcast.113, bf16[64,512]{1,0:T(8,128)(2,1)S(1)} %reshape.164, bf16[64,512]{1,0:T(8,128)(2,1)S(1)} %reshape.162), kind=kOutput, calls=%fused_computation.98 | convolution fusion | flops 537133056 | bytes 9568256 | tf_op jit(solution)/shard_map/dot_general | solution.py:147
  217.7 17.4 %all-reduce.2.cloned.1.call-done = f32[64,4096]{1,0:T(8,128)} async-done(((f32[64,4096]{1,0:T(8,128)}), f32[64,4096]{1,0:T(8,128)}) %all-reduce.2.cloned.1.call-update) | async-done | bytes 1048592 | tf_op jit(solution)/shard_map/psum | solution.py:154
  235.1 1.2 multiply_reduce_fusion
  236.3 1.5 convolution_convert_fusion
  238.0 43.0 %all_to_all.10 = bf16[8,18,4096]{2,1,0:T(8,128)(2,1)S(1)} all-to-all(bf16[8,18,4096]{2,1,0:T(8,128)(2,1)S(1)} %bitcast.114), channel_id=1, replica_groups=mesh['grp'=2,'tok'=8,'mdl'=2] {'tok'}, dimensions={0} | all-to-all | bytes 2359296 | tf_op jit(solution)/shard_map/all_to_all | solution.py:177
  281.0 1.7 copy.77
  282.9 9.9 %all-gather.9.cloned.1.call-done = bf16[8,36,4096]{2,0,1:T(8,128)(2,1)} async-done(((bf16[8,18,4096]{2,0,1:T(8,128)(2,1)}), bf16[8,36,4096]{2,0,1:T(8,128)(2,1)}) %all-gather.9.cloned.1.call-update) | async-done | bytes 2359312 | tf_op jit(solution)/shard_map/all_gather | solution.py:180
  292.8 3.0 copy.78
  295.8 2.1 reshape_reshape.6
  297.9 9.1 %fusion.54 = f32[288,1792]{1,0:T(8,128)S(1)} fusion(bf16[288,4096]{1,0:T(8,128)(2,1)} %reshape_reshape.6, bf16[1,4096,1792]{2,1,0:T(8,128)(2,1)} %param.29), kind=kOutput, calls=%fused_computation.62 | convolution fusion | flops 4227858432 | bytes 19103744 | tf_op jit(solution)/shard_map/dot_general | solution.py:183
  307.1 9.9 %fusion.66 = bf16[288,1792]{1,0:T(8,128)(2,1)S(1)} fusion(bf16[288,4096]{1,0:T(8,128)(2,1)S(1)} %copy-done.4, bf16[1,4096,1792]{2,1,0:T(8,128)(2,1)} %param.30, f32[288,1792]{1,0:T(8,128)S(1)} %fusion.54), kind=kOutput, calls=%fused_computation.73 | convolution fusion | flops 4230955008 | bytes 20135936 | tf_op jit(solution)/shard_map/dot_general | solution.py:184
  317.0 5.7 %fusion.56 = bf16[288,4096]{1,0:T(8,128)(2,1)} fusion(bf16[288,1792]{1,0:T(8,128)(2,1)S(1)} %fusion.66, bf16[1,1792,4096]{2,1,0:T(8,128)(2,1)S(1)} %bitcast.122), kind=kOutput, calls=%fused_computation.64 | convolution fusion | flops 4229038080 | bytes 18071552 | tf_op jit(solution)/shard_map/dot_general | solution.py:186
  322.7 2.7 reshape_reshape.7
  325.5 2.7 copy.79
  328.2 11.4 %reduce-scatter.2.cloned.1.call-done = bf16[8,1,18,4096]{3,0,2,1:T(8,128)(2,1)} async-done(((bf16[8,2,18,4096]{3,0,2,1:T(8,128)(2,1)}), bf16[8,1,18,4096]{3,0,2,1:T(8,128)(2,1)}) %reduce-scatter.2.cloned.1.call-update) | async-done | bytes 1179664 | tf_op jit(solution)/shard_map/reduce_scatter | solution.py:191
  339.6 3.2 copy.80
  342.8 5.9 %all-to-all-start.1 = ((bf16[8,18,4096]{2,1,0:T(8,128)(2,1)}), bf16[8,18,4096]{2,1,0:T(8,128)(2,1)S(1)}, u32[]{:S(2)}, u32[]{:S(2)}) async-start(bf16[8,18,4096]{2,1,0:T(8,128)(2,1)} %copy.80), calls=%async_computation.2 | async-start | bytes 3145728 | tf_op jit(solution)/shard_map/all_to_all | solution.py:194
  348.8 0.7 copy.83
  349.5 36.6 %all-to-all-done.1 = bf16[8,18,4096]{2,1,0:T(8,128)(2,1)S(1)} async-done(((bf16[8,18,4096]{2,1,0:T(8,128)(2,1)}), bf16[8,18,4096]{2,1,0:T(8,128)(2,1)S(1)}, u32[]{:S(2)}, u32[]{:S(2)}) %all-to-all-start.1) | async-done | bytes 1179680 | tf_op jit(solution)/shard_map/all_to_all | solution.py:194
  386.0 0.3 convert_reduce_fusion
  386.3 1.6 fusion.60
  (86 shorter events, 4.1 us)
Async XLA Ops:
  7.2 5.9 %copy-start.5 = (bf16[64,8,128]{2,1,0:T(8,128)(2,1)S(1)}, bf16[64,8,128]{2,1,0:T(8,128)(2,1)}, u32[]{:S(2)}) copy-start(bf16[64,8,128]{2,1,0:T(8,128)(2,1)} %param.22) | copy-start | bytes 393220
  7.2 5.9 %copy-start.2 = (bf16[1,2048,2,2,128]{4,3,2,1,0:T(2,128)(2,1)S(1)}, bf16[1,2048,2,2,128]{4,3,2,1,0:T(2,128)(2,1)}, u32[]{:S(2)}) copy-start(bf16[1,2048,2,2,128]{4,3,2,1,0:T(2,128)(2,1)} %param.23) | copy-start | bytes 6291460
  7.2 78.5 %all-gather.5.cloned.1.call-start = ((), (), s32[]{:S(2)}) async-start(), calls=%async_computation.3 | async-start | bytes 4718592 | tf_op jit(solution)/shard_map/all_gather | solution.py:118
  7.9 203.3 %all-gather.7.cloned.1.call-start = ((), (), s32[]{:S(2)}) async-start(), calls=%async_computation.4 | async-start | bytes 9437184 | tf_op jit(solution)/shard_map/all_gather | solution.py:146
  8.7 226.4 %all-reduce.2.cloned.1.call-start = ((), (), s32[]{:S(2)}) async-start(), calls=%async_computation.5 | async-start | bytes 2097152 | tf_op jit(solution)/shard_map/psum | solution.py:154
  12.6 223.7 %copy-start = (bf16[64,4096]{1,0:T(8,128)(2,1)}, bf16[64,4096]{1,0:T(8,128)(2,1)S(1)}, u32[]{:S(2)}) copy-start(bf16[64,4096]{1,0:T(8,128)(2,1)S(1)} %all_gather.12) | copy-start | bytes 1572868
  211.2 6.2 %copy-start.7 = (s32[32,2]{0,1:T(2,128)S(1)}, s32[32,2]{0,1:T(2,128)}, u32[]{:S(2)}) copy-start(s32[32,2]{0,1:T(2,128)} %param.32) | copy-start | bytes 772
  211.2 6.4 %copy-start.6 = (bf16[4096]{0:T(1024)(128)(2,1)S(1)}, bf16[4096]{0:T(1024)(128)(2,1)}, u32[]{:S(2)}) copy-start(bf16[4096]{0:T(1024)(128)(2,1)} %param.28) | copy-start | bytes 24580
  217.3 75.5 %all-gather.9.cloned.1.call-start = ((), (), s32[]{:S(2)}) async-start(), calls=%async_computation.7 | async-start | bytes 3538944 | tf_op jit(solution)/shard_map/all_gather | solution.py:180
  282.7 57.0 %reduce-scatter.2.cloned.1.call-start = ((), (), s32[]{:S(2)}) async-start(), calls=%async_computation.6 | async-start | bytes 3538944 | tf_op jit(solution)/shard_map/reduce_scatter | solution.py:191
  297.9 9.1 %copy-start.4 = (bf16[288,4096]{1,0:T(8,128)(2,1)S(1)}, bf16[288,4096]{1,0:T(8,128)(2,1)}, u32[]{:S(2)}) copy-start(bf16[288,4096]{1,0:T(8,128)(2,1)} %reshape_reshape.6) | copy-start | bytes 7077892
  297.9 19.0 %slice-start = ((s8[14680064]{0:T(1024)(128)(4,1)}), s8[4194304]{0:T(1024)(128)(4,1)S(1)}, s32[]{:S(2)}) async-start(s8[14680064]{0:T(1024)(128)(4,1)} %bitcast.121), calls=%async_computation.8 | async-start | bytes 8388608
  297.9 19.0 %slice-start.1 = ((s8[14680064]{0:T(1024)(128)(4,1)}), s8[4194304]{0:T(1024)(128)(4,1)S(1)}, s32[]{:S(2)}) async-start(s8[14680064]{0:T(1024)(128)(4,1)} %bitcast.121), calls=%async_computation.9 | async-start | bytes 8388608
  307.1 9.9 %slice-start.2 = ((s8[14680064]{0:T(1024)(128)(4,1)}), s8[4194304]{0:T(1024)(128)(4,1)S(1)}, s32[]{:S(2)}) async-start(s8[14680064]{0:T(1024)(128)(4,1)} %bitcast.121), calls=%async_computation.10 | async-start | bytes 8388608
  307.1 9.9 %slice-start.3 = ((s8[14680064]{0:T(1024)(128)(4,1)}), s8[2097152]{0:T(1024)(128)(4,1)S(1)}, s32[]{:S(2)}) async-start(s8[14680064]{0:T(1024)(128)(4,1)} %bitcast.121), calls=%async_computation.11 | async-start | bytes 4194304
  339.6 9.1 %copy-start.8 = (f32[32,2]{0,1:T(2,128)S(1)}, f32[32,2]{0,1:T(2,128)}, u32[]{:S(2)}) copy-start(f32[32,2]{0,1:T(2,128)} %param.33) | copy-start | bytes 772
  342.8 43.2 %all-to-all-start.1 = ((bf16[8,18,4096]{2,1,0:T(8,128)(2,1)}), bf16[8,18,4096]{2,1,0:T(8,128)(2,1)S(1)}, u32[]{:S(2)}, u32[]{:S(2)}) async-start(bf16[8,18,4096]{2,1,0:T(8,128)(2,1)} %copy.80), calls=%async_computation.2 | async-start | bytes 3145728 | tf_op jit(solution)/shard_map/all_to_all | solution.py:194
  348.7 37.6 %copy-start.1 = (bf16[64,4096]{1,0:T(8,128)(2,1)S(1)}, bf16[64,4096]{1,0:T(8,128)(2,1)}, u32[]{:S(2)}) copy-start(bf16[64,4096]{1,0:T(8,128)(2,1)} %copy-done) | copy-start | bytes 1572868
  348.7 37.6 %copy-start.3 = (f32[64,4096]{1,0:T(8,128)S(1)}, f32[64,4096]{1,0:T(8,128)}, u32[]{:S(2)}) copy-start(f32[64,4096]{1,0:T(8,128)} %all-reduce.2.cloned.1.call-done) | copy-start | bytes 3145732
Sparse Core Ops, SparseCore 0:
  10.1 75.5 all-gather.4
  87.7 123.4 all-gather.6
  217.4 17.5 all-reduce.1
  282.8 9.9 all-gather.8
  328.3 11.2 reduce-scatter.1
where the time goes:
time: 395 us; the launch traced here: 394 us
  waiting for transfers between devices  246 us (62%)
  blocking collectives  45.5 us (12%)
  matrix products  41.5 us (11%)
  local copies, waits for them, and re-layouts  31.2 us (8%)
  between operations  14.8 us (4%)
  other arithmetic  8.92 us (2%)
  starting transfers between devices  6.27 us (2%)
    all_gather x1, waiting for transfers between devices, shards(): weight_piece = lax.all_gather(wo, 'tok', axis=2, tiled=True)  99.9 us
    all_gather x1, waiting for transfers between devices, shards(): weight_piece = lax.all_gather(wkv, 'tok', axis=0, tiled=True)  69.3 us
    all_to_all x1, blocking collectives, shards(): lax.all_to_all(send_chip, 'tok', split_axis=0, concat_axis=0, tiled=True)  43 us
    all_to_all x1, waiting for transfers between devices, shards(): lax.all_to_all(chip_total[:, 0].astype(jnp.bfloat16), 'tok', split_axis=0...  36.6 us
    psum x1, waiting for transfers between devices, shards(): summed_heads = lax.psum(attn_out, 'mdl')  17.4 us
    reduce_scatter x1, waiting for transfers between devices, shards(): lax.psum_scatter(per_core.astype(jnp.bfloat16), 'mdl', scatter_dimension=...  11.4 us
    reshape x1, local copies, waits for them, and re-layouts, shards(): weight_piece.reshape(weight_piece.shape[0], -1)  11.3 us
    all_gather x1, waiting for transfers between devices, shards(): both_cores = lax.all_gather(received[:, None], 'mdl', axis=1, tiled=True)  9.91 us
  transfers between devices with their start and end apart: 6, of which 6 were waited for; matrix products, arithmetic and copies ran while one was open for 8% of the time, Pallas kernels for 0%

commit v1 on v0

--- a/solution.py
+++ b/solution.py
@@ -1,8 +1,11 @@
+import functools
 import math
 
 import jax
 import jax.numpy as jnp
 from jax import lax
+from jax.experimental import pallas as pl
+from jax.experimental.pallas import tpu as pltpu
 from jax.sharding import PartitionSpec as P
 
 EXPERTS = 4
@@ -93,6 +96,196 @@
 
     total = lax.fori_loop(0, block_total, second_pass, start_total)
     return total.astype(jnp.bfloat16)
+
+
+MESH = pl.DeviceIdType.MESH
+VMEM = pl.BlockSpec(memory_space=pltpu.VMEM)
+
+
+def place(tok, mdl):
+    return (lax.axis_index("grp"), tok, mdl)
+
+
+def greet(peers):
+    barrier = pltpu.get_barrier_semaphore()
+    for peer in peers:
+        pl.semaphore_signal(barrier, inc=1, device_id=peer, device_id_type=MESH)
+    pl.semaphore_wait(barrier, len(peers))
+
+
+def peers_of(groups, ranks, cores):
+    tok, mdl = lax.axis_index("tok"), lax.axis_index("mdl")
+    group, rank = tok // ranks, tok % ranks
+    peers = [place((group + d) % groups * ranks + rank, mdl) for d in range(1, groups)]
+    peers += [place(group * ranks + (rank + d) % ranks, mdl) for d in range(1, ranks)]
+    if cores:
+        peers.append(place(tok, 1 - mdl))
+    return peers
+
+
+def remote(src, dst, sems, index, device):
+    copy = pltpu.make_async_remote_copy(
+        src_ref=src,
+        dst_ref=dst,
+        send_sem=sems.at[0, index],
+        recv_sem=sems.at[1, index],
+        device_id=device,
+        device_id_type=MESH,
+    )
+    copy.start()
+    return copy
+
+
+def spread_kernel(groups, ranks, cores, same, send, out, sems, local_sem):
+    tok, mdl = lax.axis_index("tok"), lax.axis_index("mdl")
+    group, rank = tok // ranks, tok % ranks
+    greet(peers_of(groups, ranks, cores))
+
+    def piece(index):
+        return send if same else send.at[index]
+
+    def slot(index):
+        return out.at[index, mdl] if cores else out.at[index]
+
+    started = []
+    count = [0]
+
+    def go(src, dst, device):
+        copy = remote(src, dst, sems, count[0], device)
+        count[0] += 1
+        started.append(copy)
+        return copy
+
+    own = pltpu.make_async_copy(piece(group), slot(tok), local_sem)
+    own.start()
+    first = {}
+    for d in range(1, groups):
+        there = (group + d) % groups
+        first[d] = go(piece(there), slot(tok), place(there * ranks + rank, mdl))
+    second, third = [], []
+
+    def onward(src, index):
+        for d in range(1, ranks):
+            there = group * ranks + (rank + d) % ranks
+            second.append((d, index, go(src, slot(index), place(there, mdl))))
+
+    def across(src, index):
+        if cores:
+            third.append(go(src, slot(index), place(tok, 1 - mdl)))
+
+    onward(piece(group), tok)
+    across(piece(group), tok)
+    for d in range(1, groups):
+        first[d].wait_recv()
+        index = (group + groups - d) % groups * ranks + rank
+        onward(slot(index), index)
+        across(slot(index), index)
+    for d, index, copy in second:
+        copy.wait_recv()
+        index = index // ranks * ranks + (rank + ranks - d) % ranks
+        across(slot(index), index)
+    for copy in third:
+        copy.wait_recv()
+    for copy in started:
+        copy.wait_send()
+    own.wait()
+
+
+def spread(send, groups, ranks, cores, same, number):
+    tiles = send.shape if same else send.shape[1:]
+    toks = groups * ranks
+    core_count = lax.axis_size("mdl") if cores else 1
+    lead = (toks, core_count) if cores else (toks,)
+    copies = groups - 1 + groups * (ranks - 1) + (toks if cores else 0)
+    return pl.pallas_call(
+        functools.partial(spread_kernel, groups, ranks, cores, same),
+        out_shape=jax.ShapeDtypeStruct(lead + tiles, send.dtype),
+        in_specs=[VMEM],
+        out_specs=VMEM,
+        scratch_shapes=[pltpu.SemaphoreType.DMA((2, copies)), pltpu.SemaphoreType.DMA],
+        compiler_params=pltpu.CompilerParams(
+            collective_id=number, has_side_effects=True, vmem_limit_bytes=40 * 1024 * 1024
+        ),
+    )(send)
+
+
+def collect_kernel(groups, ranks, parts, out, near, held, mid, sems):
+    tok, mdl = lax.axis_index("tok"), lax.axis_index("mdl")
+    group, rank = tok // ranks, tok % ranks
+    greet(peers_of(groups, ranks, True))
+    started = []
+    count = [0]
+
+    def go(src, dst, device):
+        copy = remote(src, dst, sems, count[0], device)
+        count[0] += 1
+        started.append(copy)
+        return copy
+
+    order = [
+        (r, g)
+        for r in list(range(1, ranks)) + [0]
+        for g in list(range(1, groups)) + [0]
+    ]
+
+    def index_of(r, g):
+        return (group + g) % groups * ranks + (rank + r) % ranks
+
+    across = {}
+    for r, g in order:
+        index = index_of(r, g)
+        across[r, g] = go(parts.at[index, 1 - mdl], near.at[index], place(tok, 1 - mdl))
+    second = {}
+    for r, g in order:
+        if r == 0:
+            continue
+        index = index_of(r, g)
+        across[r, g].wait_recv()
+        both = parts[index, mdl].astype(jnp.float32) + near[index].astype(jnp.float32)
+        held[index] = both.astype(held.dtype)
+        second[r, g] = go(
+            held.at[index], mid.at[r - 1, g], place(group * ranks + (rank + r) % ranks, mdl)
+        )
+    last = []
+    for g in list(range(1, groups)) + [0]:
+        index = index_of(0, g)
+        across[0, g].wait_recv()
+        total = parts[index, mdl].astype(jnp.float32) + near[index].astype(jnp.float32)
+        for r in range(1, ranks):
+            second[r, g].wait_recv()
+            total = total + mid[r - 1, g].astype(jnp.float32)
+        if g == 0:
+            out[group] = total.astype(out.dtype)
+        else:
+            held[index] = total.astype(held.dtype)
+            last.append(
+                go(held.at[index], out.at[group], place((group + g) % groups * ranks + rank, mdl))
+            )
+    for copy in last:
+        copy.wait_recv()
+    for copy in started:
+        copy.wait_send()
+
+
+def collect(parts, groups, ranks, number):
+    toks = groups * ranks
+    tile = parts.shape[2:]
+    copies = toks + groups * (ranks - 1) + groups - 1
+    return pl.pallas_call(
+        functools.partial(collect_kernel, groups, ranks),
+        out_shape=jax.ShapeDtypeStruct((groups,) + tile, parts.dtype),
+        in_specs=[VMEM],
+        out_specs=VMEM,
+        scratch_shapes=[
+            pltpu.VMEM((toks,) + tile, parts.dtype),
+            pltpu.VMEM((toks,) + tile, parts.dtype),
+            pltpu.VMEM((max(ranks - 1, 1), groups) + tile, parts.dtype),
+            pltpu.SemaphoreType.DMA((2, copies)),
+        ],
+        compiler_params=pltpu.CompilerParams(
+            collective_id=number, has_side_effects=True, vmem_limit_bytes=40 * 1024 * 1024
+        ),
+    )(parts)
 
 
 def shards(
@@ -112,15 +305,25 @@
 ):
     full_rows = lax.all_gather(hidden, "mdl", axis=1, tiled=True)
     span_len = full_rows.shape[0]
-    normalized_input = rms_scale(full_rows, attn_gain).astype(jnp.bfloat16)
+    toks = lax.axis_size("tok")
+    core_count = lax.axis_size("mdl")
+    ranks = toks // EXPERTS
+    core_rows = span_len // core_count
+    core_start = lax.axis_index("mdl") * core_rows
+    own_rows = lax.dynamic_slice_in_dim(full_rows, core_start, core_rows, 0)
+    normalized_input = rms_scale(own_rows, attn_gain).astype(jnp.bfloat16)
     kv_heads = wkv.shape[1]
     head_dim = wkv.shape[3]
-    weight_piece = lax.all_gather(wkv, "tok", axis=0, tiled=True)
-    key_value_projection = jnp.dot(
-        normalized_input,
-        weight_piece.reshape(weight_piece.shape[0], -1),
-        preferred_element_type=jnp.float32,
-    ).reshape(span_len, kv_heads, 2, head_dim)
+    depth = wkv.shape[0]
+    slices = normalized_input.reshape(core_rows, toks, depth).transpose(1, 0, 2)
+    every_row = spread(slices, toks, 1, True, False, 1).reshape(-1, depth)
+    partial_kv = jnp.dot(
+        every_row, wkv.reshape(depth, -1), preferred_element_type=jnp.float32
+    ).astype(jnp.bfloat16)
+    terms = spread(partial_kv.reshape(toks, span_len, -1), toks, 1, False, False, 2)
+    key_value_projection = jnp.sum(terms.astype(jnp.float32), axis=0).reshape(
+        span_len, kv_heads, 2, head_dim
+    )
     length = cache_lengths[0]
     positions = length + jnp.arange(span_len, dtype=jnp.int32)
     fresh_key_value = jnp.stack(
@@ -143,20 +346,17 @@
         )
         outputs.append(attended.reshape(span_len, head_group * head_dim))
     heads_out = jnp.concatenate(outputs, axis=1)
-    weight_piece = lax.all_gather(wo, "tok", axis=2, tiled=True)
-    attn_out = jnp.dot(
-        heads_out,
-        weight_piece.reshape(-1, weight_piece.shape[2]),
+    every_head = spread(heads_out, EXPERTS, ranks, False, True, 3)
+    attn_part = jnp.dot(
+        every_head.reshape(toks * span_len, -1),
+        wo.reshape(-1, wo.shape[2]),
         preferred_element_type=jnp.float32,
-    )
-    core_rows = span_len // lax.axis_size("mdl")
-    core_start = lax.axis_index("mdl") * core_rows
-    summed_heads = lax.psum(attn_out, "mdl")
-    attn_rows = lax.dynamic_slice_in_dim(summed_heads, core_start, core_rows, 0)
-    resid = (
-        lax.dynamic_slice_in_dim(full_rows, core_start, core_rows, 0).astype(jnp.float32)
-        + attn_rows
-    )
+    ).astype(jnp.bfloat16)
+    attn_rows = collect(
+        attn_part.reshape(toks, core_count, core_rows, -1), toks, 1, 4
+    )
+    attn_rows = attn_rows.transpose(1, 0, 2).reshape(core_rows, -1).astype(jnp.float32)
+    resid = own_rows.astype(jnp.float32) + attn_rows
     moe_in = rms_scale(resid, moe_gain).astype(jnp.bfloat16)
     expert_range = jnp.arange(EXPERTS)
     matches = expert_ids[:, :, None] == expert_range[None, None, :]
@@ -169,16 +369,8 @@
     send_rows = jnp.einsum(
         "eci,id->ecd", select.astype(jnp.bfloat16), moe_in, preferred_element_type=jnp.float32
     ).astype(jnp.bfloat16)
-    owners = lax.axis_size("tok") * lax.axis_size("mdl")
-    slabs = owners // EXPERTS
     model_width = moe_in.shape[1]
-    core_count = lax.axis_size("mdl")
-    send_chip = jnp.repeat(send_rows, slabs // core_count, axis=0)
-    received = lax.all_to_all(send_chip, "tok", split_axis=0, concat_axis=0, tiled=True)
-    chip_count = received.shape[0]
-    item_count = received.shape[1]
-    both_cores = lax.all_gather(received[:, None], "mdl", axis=1, tiled=True)
-    received = both_cores.reshape(-1, item_count, model_width)
+    received = spread(send_rows, EXPERTS, ranks, True, False, 5)
     flat_rows = received.reshape(-1, model_width)
     gate_val = jnp.dot(flat_rows, w_gate[0], preferred_element_type=jnp.float32)
     up_val = jnp.dot(flat_rows, w_up[0], preferred_element_type=jnp.float32)
@@ -186,15 +378,7 @@
     slab_out = jnp.dot(slab_hidden, w_down[0], preferred_element_type=jnp.float32).astype(
         jnp.bfloat16
     )
-    slab_out = slab_out.reshape(received.shape)
-    per_core = slab_out.reshape(chip_count, core_count, item_count, model_width).astype(jnp.float32)
-    chip_total = lax.psum_scatter(
-        per_core.astype(jnp.bfloat16), "mdl", scatter_dimension=1, tiled=True
-    ).astype(jnp.float32)
-    returned = lax.all_to_all(
-        chip_total[:, 0].astype(jnp.bfloat16), "tok", split_axis=0, concat_axis=0, tiled=True
-    ).astype(jnp.float32)
-    summed = jnp.sum(returned.reshape(EXPERTS, slabs // core_count, capacity, model_width), axis=1)
+    summed = collect(slab_out.reshape(received.shape), EXPERTS, ranks, 6).astype(jnp.float32)
     weight_table = select.astype(jnp.float32) * route.T[:, None, :]
     moe_out = jnp.einsum("eci,ecd->id", weight_table, summed, precision=lax.Precision.HIGHEST)
     mixed = (resid + moe_out).astype(jnp.bfloat16)

time: 395 us -> 214 us (0.54)
  waiting for transfers between devices: 246 us -> 0 us
  Pallas kernels: 0 us -> 122 us
  blocking collectives: 45.5 us -> 2.51 us
  local copies, waits for them, and re-layouts: 31.2 us -> 17.4 us
  between operations: 14.8 us -> 1.98 us
  other arithmetic: 8.92 us -> 20 us
  matrix products: 41.5 us -> 48.7 us
  starting transfers between devices: 6.27 us -> 0 us
    all_gather x3 -> x0, waiting for transfers between devices: 179 us -> none  [the longest x1 99.9 us: shards(): weight_piece = lax.all_gather(wo, 'tok', axis=2, tiled=True)]
    pallas_call x0 -> x6, Pallas kernels: none -> 122 us  [the longest x4 79.4 us: spread(): pl.pallas_call(functools.partial(spread_kernel, groups, ranks, cores, sam...]
    all_to_all x1 -> x0, blocking collectives: 43 us -> none  [shards(): lax.all_to_all(send_chip, 'tok', split_axis=0, concat_axis=0, tiled=True)]
    all_to_all x1 -> x0, waiting for transfers between devices: 36.6 us -> none  [shards(): lax.all_to_all(chip_total[:, 0].astype(jnp.bfloat16), 'tok', split_axis=0...]
    psum x1 -> x0, waiting for transfers between devices: 17.4 us -> none  [shards(): summed_heads = lax.psum(attn_out, 'mdl')]
    reduce_scatter x1 -> x0, waiting for transfers between devices: 11.4 us -> none  [shards(): lax.psum_scatter(per_core.astype(jnp.bfloat16), 'mdl', scatter_dimension=...]
    dot_general x4 -> x8, matrix products: 2.18 us -> 12.1 us  [second_pass(): jnp.dot(probs, block_values, preferred_element_type=jnp.float32)]
    dot_general x2, matrix products: 9.77 us -> 1.15 us  [the longest x1 0.71 us: shards(): jnp.dot(every_head.reshape(toks * span_len, -1), wo.reshape(-1, wo.shape[...]
  transfers between devices with their start and end apart: 6 -> 0, of which waited for: 6 -> 0; matrix products, arithmetic and copies ran while one was open for 8% -> 0% of each run, Pallas kernels for 0% -> 0%
where the time goes in v1:
time: 214 us
  Pallas kernels  122 us (57%)
  matrix products  48.7 us (23%)
  other arithmetic  20 us (9%)
  local copies, waits for them, and re-layouts  17.4 us (8%)
  blocking collectives  2.51 us (1%)
    pallas_call x4, Pallas kernels, spread(): pl.pallas_call(functools.partial(spread_kernel, groups, ranks, cores, sam...  79.4 us
    pallas_call x2, Pallas kernels, collect(): pl.pallas_call(functools.partial(collect_kernel, groups, ranks), out_shap...  43 us
    dot_general x8, matrix products, second_pass(): jnp.dot(probs, block_values, preferred_element_type=jnp.float32)  12.1 us
    lt x16, other arithmetic, block_scores(): allowed = row_offset + jnp.arange(block_len) < length  10.6 us
    dot_general x1, matrix products, shards(): up_val = jnp.dot(flat_rows, w_up[0], preferred_element_type=jnp.float32)  9.85 us
    dot_general x10, matrix products, score_rows(): lax.dot_general(query_rows, key_rows, (((1,), (1,)), ((), ())), preferred...  9.74 us
    dot_general x1, matrix products, shards(): gate_val = jnp.dot(flat_rows, w_gate[0], preferred_element_type=jnp.float32)  9.13 us
    dot_general x1, matrix products, shards(): jnp.dot(slab_hidden, w_down[0], preferred_element_type=jnp.float32)  4.64 us

profile of v1, /device:TPU:0, one launch (start us, length us, event | category | flops | bytes accessed | tf_op | source)
XLA Modules:
  0.0 213.6 jit_solution(5171894184918506884)
XLA Ops:
  1.9 0.7 convert_reduce_fusion.1
  3.1 1.3 select_reduce_fusion.4
  5.2 0.7 convert_element_type.79
  5.9 1.3 convert_element_type.93
  7.2 0.8 multiply_cosine_fusion
  8.0 1.0 fusion.110
  9.1 2.5 %all_gather.3 = bf16[64,4096]{1,0:T(8,128)(2,1)S(1)} all-gather(bf16[64,2048]{1,0:T(8,128)(2,1)} %param.21), channel_id=1, replica_groups=mesh['grp'=2,'tok'=8,'mdl'=2] {'mdl'}, dimensions={1}, use_global_device_ids=true | all-gather | bytes 786432 | tf_op jit(solution)/shard_map/all_gather | solution.py:306
  12.4 12.2 %shard_map.140 = bf16[8,2,32,512]{3,2,1,0:T(8,128)(2,1)S(1)} custom-call(bf16[8,32,512]{2,1,0:T(8,128)(2,1)S(1)} %bitcast.111), custom_call_target="tpu_custom_call" | custom-call | tf_op jit(solution)/shard_map/pallas_call | solution.py:200
  25.2 14.3 %shard_map.141 = bf16[8,64,512]{2,1,0:T(8,128)(2,1)S(1)} custom-call(bf16[8,64,512]{2,1,0:T(8,128)(2,1)S(1)} %bitcast.110), custom_call_target="tpu_custom_call" | custom-call | tf_op jit(solution)/shard_map/pallas_call | solution.py:200
  39.8 0.9 subtract_convert_fusion
  41.0 0.8 pad_maximum_fusion.1
  41.8 0.7 fusion.111
  42.9 3.9 %fusion.109 = (bf16[1,2048,1,1,128]{4,3,2,1,0:T(2,128)(2,1)S(1)}, bf16[1,2048,1,1,128]{4,3,2,1,0:T(2,128)(2,1)}, bf16[1,2048,1,1,128]{4,3,2,1,0:T(2,128)(2,1)S(1)}, bf16[1,2048,1,1,128]{4,3,2,1,0:T(2,128)(2,1)}) fusion(bf16[1,2048,2,2,128]{4,3,2,1,0:T(2,128)(2,1)S(1)} %copy-done.5), kind=kLoop, calls=%fused_computation.155 | loop fusion | bytes 4194304 | tf_op jit(solution)/shard_map/slice | solution.py:341
  46.8 1.1 copy_bitcast_fusion.2
  48.0 8.2 %while.44 = (s32[]{:T(128)}, f32[256]{0:T(256)S(1)}, f32[256]{0:T(256)S(1)}, s32[]{:T(128)}, s32[]{:T(128)}, /*index=5*/bf16[2048,128]{1,0:T(8,128)(2,1)}, bf16[...) while((s32[]{:T(128)}, f32[256]{0:T(256)S(1)}, f32[256]{0:T(256)S(1)}, ...), condition=%wide.region_7.8_spmd, body=%wide.region_4.7_spmd.sunk | while | flops 34342404 | bytes 1260199 | solution.py:83
  48.6 1.2 fusion.141
  50.7 1.2 fusion.141
  52.7 1.2 fusion.141
  54.8 1.2 fusion.141
  56.4 8.9 %while.45 = (s32[]{:T(128)}, f32[256,128]{1,0:T(8,128)S(1)}, s32[]{:T(128)}, s32[]{:T(128)}, bf16[2048,128]{1,0:T(8,128)(2,1)}, /*index=5*/bf16[256,128]{1,0:T(8...) while((s32[]{:T(128)}, f32[256,128]{1,0:T(8,128)S(1)}, ...), condition=%wide.region_9.10_spmd, body=%wide.region_8.9_spmd.sunk | while | flops 67929096 | bytes 594099 | solution.py:97
  56.4 0.8 add_compare_fusion.9
  57.2 1.5 fusion.145
  59.4 1.5 fusion.145
  61.6 1.5 fusion.145
  63.8 1.5 fusion.145
  65.4 1.1 copy_bitcast_fusion
  66.5 8.2 %while.46 = (s32[]{:T(128)}, f32[256]{0:T(256)S(1)}, f32[256]{0:T(256)S(1)}, s32[]{:T(128)}, s32[]{:T(128)}, /*index=5*/bf16[2048,128]{1,0:T(8,128)(2,1)}, bf16[...) while((s32[]{:T(128)}, f32[256]{0:T(256)S(1)}, f32[256]{0:T(256)S(1)}, ...), condition=%wide.region_15.16_spmd, body=%wide.region_12.15_spmd.sunk | while | flops 34342404 | bytes 1260199 | solution.py:83
  67.2 1.2 fusion.147
  69.3 1.2 fusion.147
  71.3 1.2 fusion.147
  73.3 1.2 fusion.147
  74.9 9.0 %while.47 = (s32[]{:T(128)}, f32[256,128]{1,0:T(8,128)S(1)}, s32[]{:T(128)}, s32[]{:T(128)}, bf16[2048,128]{1,0:T(8,128)(2,1)}, /*index=5*/bf16[256,128]{1,0:T(8...) while((s32[]{:T(128)}, f32[256,128]{1,0:T(8,128)S(1)}, ...), condition=%wide.region_17.18_spmd, body=%wide.region_16.17_spmd.sunk | while | flops 67929096 | bytes 594099 | solution.py:97
  75.6 1.5 fusion.151
  77.8 1.5 fusion.151
  80.0 1.5 fusion.151
  82.2 1.5 fusion.151
  84.0 23.3 %shard_map.142 = bf16[8,64,1024]{2,1,0:T(8,128)(2,1)S(1)} custom-call(bf16[64,1024]{1,0:T(8,128)(2,1)S(1)} %pad_maximum_fusion.send), custom_call_target="tpu_custom_call" | custom-call | tf_op jit(solution)/shard_map/pallas_call | solution.py:200
  107.3 0.7 convolution_convert_fusion.2
  108.1 10.6 %shard_map.143 = bf16[8,32,512]{2,1,0:T(8,128)(2,1)S(1)} custom-call(bf16[8,2,32,512]{3,2,1,0:T(8,128)(2,1)S(1)} %bitcast.113), custom_call_target="tpu_custom_call" | custom-call | tf_op jit(solution)/shard_map/pallas_call | solution.py:274
  120.0 29.6 %shard_map.144 = bf16[8,2,18,4096]{3,2,1,0:T(8,128)(2,1)S(1)} custom-call(bf16[4,18,4096]{2,1,0:T(8,128)(2,1)S(1)} %convolution_convert_fusion.send), custom_call_target="tpu_custom_call" | custom-call | tf_op jit(solution)/shard_map/pallas_call | solution.py:200
  149.6 2.3 %reshape.187 = bf16[288,4096]{1,0:T(8,128)(2,1)} reshape(bf16[8,2,18,4096]{3,2,1,0:T(8,128)(2,1)S(1)} %shard_map.144) | data formatting | bytes 4718592 | tf_op jit(solution)/shard_map/reshape | solution.py:374
  151.9 9.1 %fusion.54 = f32[288,1792]{1,0:T(8,128)S(1)} fusion(bf16[288,4096]{1,0:T(8,128)(2,1)} %reshape.187, bf16[1,4096,1792]{2,1,0:T(8,128)(2,1)} %param.29), kind=kOutput, calls=%fused_computation.62 | convolution fusion | flops 4227858432 | bytes 19103744 | tf_op jit(solution)/shard_map/dot_general | solution.py:375
  161.0 9.9 %fusion.64 = bf16[288,1792]{1,0:T(8,128)(2,1)S(1)} fusion(bf16[288,4096]{1,0:T(8,128)(2,1)S(1)} %copy-done.11, bf16[1,4096,1792]{2,1,0:T(8,128)(2,1)} %param.30, f32[288,1792]{1,0:T(8,128)S(1)} %fusion.54), kind=kOutput, calls=%fused_computation.70 | convolution fusion | flops 4230955008 | bytes 20135936 | tf_op jit(solution)/shard_map/dot_general | solution.py:376
  170.9 4.6 %fusion.56 = bf16[288,4096]{1,0:T(8,128)(2,1)S(1)} fusion(bf16[288,1792]{1,0:T(8,128)(2,1)S(1)} %fusion.64, bf16[1,1792,4096]{2,1,0:T(8,128)(2,1)S(1)} %bitcast.128), kind=kOutput, calls=%fused_computation.64 | convolution fusion | flops 4229038080 | bytes 18071552 | tf_op jit(solution)/shard_map/dot_general | solution.py:378
  175.6 2.4 %reshape.188.parts = bf16[8,2,18,4096]{3,2,1,0:T(8,128)(2,1)} reshape(bf16[288,4096]{1,0:T(8,128)(2,1)S(1)} %fusion.56) | data formatting | bytes 4718592 | tf_op jit(solution)/shard_map/reshape | solution.py:381
  178.0 1.9 copy-done.2
  179.9 32.4 %shard_map.145 = bf16[4,18,4096]{2,1,0:T(8,128)(2,1)S(1)} custom-call(bf16[8,2,18,4096]{3,2,1,0:T(8,128)(2,1)S(1)} %copy-done.2), custom_call_target="tpu_custom_call" | custom-call | tf_op jit(solution)/shard_map/pallas_call | solution.py:274
  212.4 1.2 fusion.60
  (136 shorter events, 17.3 us)
Async XLA Ops:
  0.6 1.2 copy-start
  0.6 23.9 %copy-start.12 = (bf16[512,2,2,128]{3,2,1,0:T(2,128)(2,1)S(1)}, bf16[512,2,2,128]{3,2,1,0:T(2,128)(2,1)}, u32[]{:S(2)}) copy-start(bf16[512,2,2,128]{3,2,1,0:T(2,128)(2,1)} %param.25) | copy-start | bytes 1572868
  1.9 41.0 %copy-start.17 = (s32[256]{0:T(256)}, s32[256]{0:T(256)S(1)}, u32[]{:S(2)}) copy-start(s32[256]{0:T(256)S(1)} %and_select_fusion) | copy-start | bytes 3076
  11.6 0.8 copy-start.6
  25.2 17.7 %copy-start.5 = (bf16[1,2048,2,2,128]{4,3,2,1,0:T(2,128)(2,1)S(1)}, bf16[1,2048,2,2,128]{4,3,2,1,0:T(2,128)(2,1)}, u32[]{:S(2)}) copy-start(bf16[1,2048,2,2,128]{4,3,2,1,0:T(2,128)(2,1)} %param.23) | copy-start | bytes 6291460
  48.0 8.2 %copy-start.15 = (bf16[64,1,1,128]{3,2,1,0:T(2,128)(2,1)S(1)}, bf16[64,1,1,128]{3,2,1,0:T(2,128)(2,1)}, u32[]{:S(2)}) copy-start(bf16[64,1,1,128]{3,2,1,0:T(2,128)(2,1)} %get-tuple-element.262) | copy-start | bytes 49156
  48.0 8.2 %copy-start.18 = (s32[256]{0:T(256)S(1)}, s32[256]{0:T(256)}, u32[]{:S(2)}) copy-start(s32[256]{0:T(256)} %copy-done.17) | copy-start | bytes 3076
  56.4 9.1 %copy-start.9 = (bf16[1,2048,1,1,128]{4,3,2,1,0:T(2,128)(2,1)S(1)}, bf16[1,2048,1,1,128]{4,3,2,1,0:T(2,128)(2,1)}, u32[]{:S(2)}) copy-start(bf16[1,2048,1,1,128]{4,3,2,1,0:T(2,128)(2,1)} %get-tuple-element.255) | copy-start | bytes 1572868
  56.4 9.1 %copy-start.10 = (bf16[1,2048,1,1,128]{4,3,2,1,0:T(2,128)(2,1)S(1)}, bf16[1,2048,1,1,128]{4,3,2,1,0:T(2,128)(2,1)}, u32[]{:S(2)}) copy-start(bf16[1,2048,1,1,128]{4,3,2,1,0:T(2,128)(2,1)} %get-tuple-element.257) | copy-start | bytes 1572868
  66.5 8.2 %copy-start.14 = (bf16[64,1,1,128]{3,2,1,0:T(2,128)(2,1)S(1)}, bf16[64,1,1,128]{3,2,1,0:T(2,128)(2,1)}, u32[]{:S(2)}) copy-start(bf16[64,1,1,128]{3,2,1,0:T(2,128)(2,1)} %get-tuple-element.263) | copy-start | bytes 49156
  66.5 8.2 %copy-start.19 = (s32[256]{0:T(256)S(1)}, s32[256]{0:T(256)}, u32[]{:S(2)}) copy-start(s32[256]{0:T(256)} %copy-done.17) | copy-start | bytes 3076
  107.3 11.4 %copy-start.7 = (bf16[64,4096]{1,0:T(8,128)(2,1)S(1)}, bf16[64,4096]{1,0:T(8,128)(2,1)}, u32[]{:S(2)}) copy-start(bf16[64,4096]{1,0:T(8,128)(2,1)} %copy-done.6) | copy-start | bytes 1572868
  108.1 11.5 %copy-start.13 = (f32[4096]{0:T(1024)S(1)}, f32[4096]{0:T(1024)}, u32[]{:S(2)}) copy-start(f32[4096]{0:T(1024)} %convert_element_type.93) | copy-start | bytes 49156
  108.1 11.5 %copy-start.16 = (s32[4,32]{1,0:T(4,128)S(1)}, s32[4,32]{1,0:T(4,128)}, u32[]{:S(2)}) copy-start(s32[4,32]{1,0:T(4,128)} %copy.67) | copy-start | bytes 1540
  108.1 11.5 %copy-start.21 = (pred[4,32]{1,0:T(4,128)(4,1)S(1)}, pred[4,32]{1,0:T(4,128)(4,1)}, u32[]{:S(2)}) copy-start(pred[4,32]{1,0:T(4,128)(4,1)} %compare_bitcast_fusion) | copy-start | bytes 388
  118.8 0.8 copy-start.3
  151.9 9.1 %copy-start.11 = (bf16[288,4096]{1,0:T(8,128)(2,1)S(1)}, bf16[288,4096]{1,0:T(8,128)(2,1)}, u32[]{:S(2)}) copy-start(bf16[288,4096]{1,0:T(8,128)(2,1)} %reshape.187) | copy-start | bytes 7077892
  151.9 19.0 %slice-start = ((s8[14680064]{0:T(1024)(128)(4,1)}), s8[4194304]{0:T(1024)(128)(4,1)S(1)}, s32[]{:S(2)}) async-start(s8[14680064]{0:T(1024)(128)(4,1)} %bitcast.127), calls=%async_computation | async-start | bytes 8388608
  151.9 19.0 %slice-start.1 = ((s8[14680064]{0:T(1024)(128)(4,1)}), s8[4194304]{0:T(1024)(128)(4,1)S(1)}, s32[]{:S(2)}) async-start(s8[14680064]{0:T(1024)(128)(4,1)} %bitcast.127), calls=%async_computation.1 | async-start | bytes 8388608
  161.0 9.9 %slice-start.2 = ((s8[14680064]{0:T(1024)(128)(4,1)}), s8[4194304]{0:T(1024)(128)(4,1)S(1)}, s32[]{:S(2)}) async-start(s8[14680064]{0:T(1024)(128)(4,1)} %bitcast.127), calls=%async_computation.2 | async-start | bytes 8388608
  161.0 9.9 %slice-start.3 = ((s8[14680064]{0:T(1024)(128)(4,1)}), s8[2097152]{0:T(1024)(128)(4,1)S(1)}, s32[]{:S(2)}) async-start(s8[14680064]{0:T(1024)(128)(4,1)} %bitcast.127), calls=%async_computation.3 | async-start | bytes 4194304
  175.6 38.0 %copy-start.1 = (bf16[8,128,512]{2,1,0:T(8,128)(2,1)S(1)}, bf16[8,128,512]{2,1,0:T(8,128)(2,1)}, u32[]{:S(2)}) copy-start(bf16[8,128,512]{2,1,0:T(8,128)(2,1)} %param.26) | copy-start | bytes 3145732
  178.0 1.9 copy-start.2
  179.9 32.4 %copy-start.4 = (f32[8,4,8,512]{3,2,0,1:T(8,128)S(1)}, f32[8,4,8,512]{3,2,0,1:T(8,128)}, u32[]{:S(2)}) copy-start(f32[8,4,8,512]{3,2,0,1:T(8,128)} %copy-done.3) | copy-start | bytes 1572868
  179.9 32.4 %copy-start.8 = (bf16[64,4096]{1,0:T(8,128)(2,1)S(1)}, bf16[64,4096]{1,0:T(8,128)(2,1)}, u32[]{:S(2)}) copy-start(bf16[64,4096]{1,0:T(8,128)(2,1)} %copy-done.6) | copy-start | bytes 1572868
  179.9 32.4 %copy-start.20 = (f32[32,4]{0,1:T(4,128)S(1)}, f32[32,4]{0,1:T(4,128)}, u32[]{:S(2)}) copy-start(f32[32,4]{0,1:T(4,128)} %select_reduce_fusion.4) | copy-start | bytes 1540

commit v2 on v1

v2 whole, which is shorter than its diff:
```python
import functools
import math

import jax
import jax.numpy as jnp
from jax import lax
from jax.experimental import pallas as pl
from jax.experimental.pallas import tpu as pltpu
from jax.sharding import PartitionSpec as P

EXPERTS = 4
TOPK = 2


eps_norm = 1e-05
rope_base = 1000000.0
mask_fill = -1e30


def rms_scale(values_in, gain):
    values = values_in.astype(jnp.float32)
    meansq = jnp.mean(values * values, axis=-1, keepdims=True)
    return values * lax.rsqrt(meansq + eps_norm) * gain.astype(jnp.float32)


def rotate(key_rows, positions):
    half_dim = key_rows.shape[-1] // 2
    inverse = jnp.exp(
        jnp.arange(half_dim, dtype=jnp.float32) * (-2.0 * math.log(rope_base) / key_rows.shape[-1])
    )
    angle = positions.astype(jnp.float32)[:, None] * inverse[None, :]
    cosine = jnp.cos(angle)[:, None, :]
    sine_vals = jnp.sin(angle)[:, None, :]
    front_half = key_rows[..., :half_dim]
    back_half = key_rows[..., half_dim:]
    return jnp.concatenate(
        [front_half * cosine - back_half * sine_vals, back_half * cosine + front_half * sine_vals],
        axis=-1,
    )


def score_rows(query_rows, key_rows, scale_factor):
    return (
        lax.dot_general(
            query_rows, key_rows, (((1,), (1,)), ((), ())), preferred_element_type=jnp.float32
        )
        * scale_factor
    )


MESH = pl.DeviceIdType.MESH
VMEM = pl.BlockSpec(memory_space=pltpu.VMEM)


def place(tok, mdl):
    return (lax.axis_index("grp"), tok, mdl)


def greet(peers):
    barrier = pltpu.get_barrier_semaphore()
    for peer in peers:
        pl.semaphore_signal(barrier, inc=1, device_id=peer, device_id_type=MESH)
    pl.semaphore_wait(barrier, len(peers))


def peers_of(groups, ranks, cores):
    tok, mdl = lax.axis_index("tok"), lax.axis_index("mdl")
    group, rank = tok // ranks, tok % ranks
    peers = [place((group + d) % groups * ranks + rank, mdl) for d in range(1, groups)]
    peers += [place(group * ranks + (rank + d) % ranks, mdl) for d in range(1, ranks)]
    if cores:
        peers.append(place(tok, 1 - mdl))
    return peers


def remote(src, dst, sems, index, device):
    copy = pltpu.make_async_remote_copy(
        src_ref=src,
        dst_ref=dst,
        send_sem=sems.at[0, index],
        recv_sem=sems.at[1, index],
        device_id=device,
        device_id_type=MESH,
    )
    copy.start()
    return copy


def near_first(count):
    return sorted(range(1, count), key=lambda d: (min(d, count - d), d))


def cut(width, pieces):
    part = width // pieces
    return [pl.ds(c * part, part) for c in range(pieces)]


def spread_kernel(groups, ranks, cores, same, pieces, send, out, sems, local_sem):
    tok, mdl = lax.axis_index("tok"), lax.axis_index("mdl")
    group, rank = tok // ranks, tok % ranks
    columns = cut(send.shape[-1], pieces)
    greet(peers_of(groups, ranks, cores))

    def piece(index, c):
        return send.at[:, columns[c]] if same else send.at[index, :, columns[c]]

    def slot(index, c):
        return out.at[index, mdl, :, columns[c]] if cores else out.at[index, :, columns[c]]

    started = []

    def go(src, dst, device):
        copy = remote(src, dst, sems, len(started), device)
        started.append(copy)
        return copy

    first, second, third = {}, [], []
    for c in range(pieces):
        for d in near_first(groups):
            there = (group + d) % groups
            first[c, d] = go(piece(there, c), slot(tok, c), place(there * ranks + rank, mdl))

    def onward(src, index, c):
        for d in near_first(ranks):
            there = group * ranks + (rank + d) % ranks
            second.append((d, index, c, go(src, slot(index, c), place(there, mdl))))

    def across(src, index, c):
        if cores:
            third.append(go(src, slot(index, c), place(tok, 1 - mdl)))

    for c in range(pieces):
        onward(piece(group, c), tok, c)
    for c in range(pieces):
        across(piece(group, c), tok, c)
    own = pltpu.make_async_copy(
        send if same else send.at[group], out.at[tok, mdl] if cores else out.at[tok], local_sem
    )
    own.start()
    for c in range(pieces):
        for d in near_first(groups):
            first[c, d].wait_recv()
            index = (group + groups - d) % groups * ranks + rank
            onward(slot(index, c), index, c)
            across(slot(index, c), index, c)
    for d, index, c, copy in second:
        copy.wait_recv()
        index = index // ranks * ranks + (rank + ranks - d) % ranks
        across(slot(index, c), index, c)
    for copy in third:
        copy.wait_recv()
    for copy in started:
        copy.wait_send()
    own.wait()


def spread(send, groups, ranks, cores, same, number, pieces=1):
    tiles = send.shape if same else send.shape[1:]
    toks = groups * ranks
    core_count = lax.axis_size("mdl") if cores else 1
    lead = (toks, core_count) if cores else (toks,)
    copies = pieces * (groups - 1 + groups * (ranks - 1) + (toks if cores else 0))
    return pl.pallas_call(
        functools.partial(spread_kernel, groups, ranks, cores, same, pieces),
        out_shape=jax.ShapeDtypeStruct(lead + tiles, send.dtype),
        in_specs=[VMEM],
        out_specs=VMEM,
        scratch_shapes=[pltpu.SemaphoreType.DMA((2, copies)), pltpu.SemaphoreType.DMA],
        compiler_params=pltpu.CompilerParams(
            collective_id=number, has_side_effects=True, vmem_limit_bytes=40 * 1024 * 1024
        ),
    )(send)


def collect_kernel(groups, ranks, pieces, parts, out, near, held, mid, sems):
    tok, mdl = lax.axis_index("tok"), lax.axis_index("mdl")
    group, rank = tok // ranks, tok % ranks
    columns = cut(parts.shape[-1], pieces)
    greet(peers_of(groups, ranks, True))
    started = []

    def go(src, dst, device):
        copy = remote(src, dst, sems, len(started), device)
        started.append(copy)
        return copy

    far = near_first(groups)[::-1] + [0]
    order = [(r, g) for r in near_first(ranks) + [0] for g in far]

    def index_of(r, g):
        return (group + g) % groups * ranks + (rank + r) % ranks

    across, second, last = {}, {}, []
    for c in range(pieces):
        for r, g in order:
            index = index_of(r, g)
            across[c, r, g] = go(
                parts.at[index, 1 - mdl, :, columns[c]],
                near.at[index, :, columns[c]],
                place(tok, 1 - mdl),
            )

    def both_cores(c, r, g):
        index = index_of(r, g)
        across[c, r, g].wait_recv()
        return parts[index, mdl, :, columns[c]].astype(jnp.float32) + near[
            index, :, columns[c]
        ].astype(jnp.float32)

    def to_ranks(c):
        for r, g in order:
            if r == 0:
                continue
            index = index_of(r, g)
            held[index, :, columns[c]] = both_cores(c, r, g).astype(held.dtype)
            second[c, r, g] = go(
                held.at[index, :, columns[c]],
                mid.at[r - 1, g, :, columns[c]],
                place(group * ranks + (rank + r) % ranks, mdl),
            )

    def to_sources(c):
        for g in far:
            index = index_of(0, g)
            total = both_cores(c, 0, g)
            for r in range(1, ranks):
                second[c, r, g].wait_recv()
                total = total + mid[r - 1, g, :, columns[c]].astype(jnp.float32)
            if g == 0:
                out[group, :, columns[c]] = total.astype(out.dtype)
            else:
                held[index, :, columns[c]] = total.astype(held.dtype)
                last.append(
                    go(
                        held.at[index, :, columns[c]],
                        out.at[group, :, columns[c]],
                        place((group + g) % groups * ranks + rank, mdl),
                    )
                )

    for c in range(pieces + 1):
        if c < pieces:
            to_ranks(c)
        if c > 0:
            to_sources(c - 1)
    for copy in last:
        copy.wait_recv()
    for copy in started:
        copy.wait_send()


def collect(parts, groups, ranks, number, pieces=1):
    toks = groups * ranks
    tile = parts.shape[2:]
    copies = pieces * (toks + groups * (ranks - 1) + groups - 1)
    return pl.pallas_call(
        functools.partial(collect_kernel, groups, ranks, pieces),
        out_shape=jax.ShapeDtypeStruct((groups,) + tile, parts.dtype),
        in_specs=[VMEM],
        out_specs=VMEM,
        scratch_shapes=[
            pltpu.VMEM((toks,) + tile, parts.dtype),
            pltpu.VMEM((toks,) + tile, parts.dtype),
            pltpu.VMEM((max(ranks - 1, 1), groups) + tile, parts.dtype),
            pltpu.SemaphoreType.DMA((2, copies)),
        ],
        compiler_params=pltpu.CompilerParams(
            collective_id=number, has_side_effects=True, vmem_limit_bytes=40 * 1024 * 1024
        ),
    )(parts)


def attention_kernel(length, queries, cached, fresh, out):
    heads, span, width = queries.shape
    rows = heads * span
    query_rows = queries[...].reshape(rows, width)
    scale_factor = 1.0 / math.sqrt(width)
    limit = cached.shape[2]
    block = min(512, limit)
    token = lax.broadcasted_iota(jnp.int32, (rows, span), 0) % span
    column = lax.broadcasted_iota(jnp.int32, (rows, span), 1)
    scores = [
        jnp.where(
            column <= token, score_rows(query_rows, fresh[0, 0], scale_factor), mask_fill
        )
    ]
    values = [fresh[0, 1]]
    for start in range(0, limit, block):
        position = lax.broadcasted_iota(jnp.int32, (rows, block), 1) + start
        found = score_rows(query_rows, cached[0, 0, pl.ds(start, block)], scale_factor)
        scores.append(jnp.where(position < length[0], found, mask_fill))
        values.append(cached[0, 1, pl.ds(start, block)])
    top = functools.reduce(jnp.maximum, [jnp.max(x, axis=1, keepdims=True) for x in scores])
    total = jnp.zeros((rows, 1), jnp.float32)
    mixed = jnp.zeros((rows, width), jnp.float32)
    for found, value_rows in zip(scores, values):
        weights = jnp.exp(found - top)
        total += jnp.sum(weights, axis=1, keepdims=True)
        mixed += jnp.dot(
            weights.astype(jnp.bfloat16), value_rows, preferred_element_type=jnp.float32
        )
    attended = (mixed / total).astype(out.dtype)
    for head in range(heads):
        out[:, head * width : (head + 1) * width] = attended[head * span : (head + 1) * span]


def attention(queries, cache, lengths, fresh):
    span, query_heads, width = queries.shape
    kv_heads = cache.shape[2]
    per_head = query_heads // kv_heads
    limit = cache.shape[1]
    return pl.pallas_call(
        attention_kernel,
        grid=(kv_heads,),
        out_shape=jax.ShapeDtypeStruct((span, query_heads * width), jnp.bfloat16),
        in_specs=[
            pl.BlockSpec(memory_space=pltpu.SMEM),
            pl.BlockSpec((per_head, span, width), lambda h: (h, 0, 0)),
            pl.BlockSpec((1, 2, limit, width), lambda h: (h, 0, 0, 0)),
            pl.BlockSpec((1, 2, span, width), lambda h: (h, 0, 0, 0)),
        ],
        out_specs=pl.BlockSpec((span, per_head * width), lambda h: (0, h)),
        compiler_params=pltpu.CompilerParams(vmem_limit_bytes=40 * 1024 * 1024),
    )(
        lengths,
        queries.transpose(1, 0, 2),
        cache[0].transpose(1, 2, 0, 3),
        fresh.transpose(1, 2, 0, 3),
    )


def shards(
    hidden,
    queries,
    cache,
    cache_lengths,
    wkv,
    wo,
    attn_gain,
    moe_gain,
    w_gate,
    w_up,
    w_down,
    expert_ids,
    gates,
):
    full_rows = lax.all_gather(hidden, "mdl", axis=1, tiled=True)
    span_len = full_rows.shape[0]
    toks = lax.axis_size("tok")
    core_count = lax.axis_size("mdl")
    ranks = toks // EXPERTS
    core_rows = span_len // core_count
    core_start = lax.axis_index("mdl") * core_rows
    own_rows = lax.dynamic_slice_in_dim(full_rows, core_start, core_rows, 0)
    normalized_input = rms_scale(own_rows, attn_gain).astype(jnp.bfloat16)
    kv_heads = wkv.shape[1]
    head_dim = wkv.shape[3]
    depth = wkv.shape[0]
    slices = normalized_input.reshape(core_rows, toks, depth).transpose(1, 0, 2)
    every_row = spread(slices, toks, 1, True, False, 1).reshape(-1, depth)
    partial_kv = jnp.dot(
        every_row, wkv.reshape(depth, -1), preferred_element_type=jnp.float32
    ).astype(jnp.bfloat16)
    terms = spread(partial_kv.reshape(toks, span_len, -1), toks, 1, False, False, 2)
    key_value_projection = jnp.sum(terms.astype(jnp.float32), axis=0).reshape(
        span_len, kv_heads, 2, head_dim
    )
    length = cache_lengths[0]
    positions = length + jnp.arange(span_len, dtype=jnp.int32)
    fresh_key_value = jnp.stack(
        [rotate(key_value_projection[:, :, 0], positions), key_value_projection[:, :, 1]], axis=2
    ).astype(jnp.bfloat16)
    heads_out = attention(queries, cache, cache_lengths, fresh_key_value)
    every_head = spread(heads_out, EXPERTS, ranks, False, True, 3, 2)
    attn_part = jnp.dot(
        every_head.reshape(toks * span_len, -1),
        wo.reshape(-1, wo.shape[2]),
        preferred_element_type=jnp.float32,
    ).astype(jnp.bfloat16)
    attn_rows = collect(
        attn_part.reshape(toks, core_count, core_rows, -1), toks, 1, 4
    )
    attn_rows = attn_rows.transpose(1, 0, 2).reshape(core_rows, -1).astype(jnp.float32)
    resid = own_rows.astype(jnp.float32) + attn_rows
    moe_in = rms_scale(resid, moe_gain).astype(jnp.bfloat16)
    expert_range = jnp.arange(EXPERTS)
    matches = expert_ids[:, :, None] == expert_range[None, None, :]
    chosen = jnp.sum(matches.astype(jnp.int32), axis=1)
    route = jnp.sum(jnp.where(matches, gates[:, :, None], 0.0), axis=1)
    slot_of = jnp.cumsum(chosen, axis=0) - chosen
    capacity = core_rows * TOPK * 9 // (8 * EXPERTS)
    slot_range = jnp.arange(capacity)
    select = (slot_of.T[:, None, :] == slot_range[None, :, None]) & (chosen.T[:, None, :] > 0)
    send_rows = jnp.einsum(
        "eci,id->ecd", select.astype(jnp.bfloat16), moe_in, preferred_element_type=jnp.float32
    ).astype(jnp.bfloat16)
    model_width = moe_in.shape[1]
    received = spread(send_rows, EXPERTS, ranks, True, False, 5, 4)
    flat_rows = received.reshape(-1, model_width)
    gate_val = jnp.dot(flat_rows, w_gate[0], preferred_element_type=jnp.float32)
    up_val = jnp.dot(flat_rows, w_up[0], preferred_element_type=jnp.float32)
    slab_hidden = (jax.nn.silu(gate_val) * up_val).astype(jnp.bfloat16)
    slab_out = jnp.dot(slab_hidden, w_down[0], preferred_element_type=jnp.float32).astype(
        jnp.bfloat16
    )
    summed = collect(slab_out.reshape(received.shape), EXPERTS, ranks, 6, 4).astype(jnp.float32)
    weight_table = select.astype(jnp.float32) * route.T[:, None, :]
    moe_out = jnp.einsum("eci,ecd->id", weight_table, summed, precision=lax.Precision.HIGHEST)
    mixed = (resid + moe_out).astype(jnp.bfloat16)
    return (mixed, fresh_key_value)


def solution(mesh):
    in_specs = (
        P(("grp", "tok"), "mdl"),
        P(("grp", "tok"), "mdl", None),
        P(("grp", "tok"), None, "mdl", None, None),
        P(("grp", "tok")),
        P("tok", "mdl", None, None),
        P("mdl", None, "tok"),
        P(),
        P(),
        P(("tok", "mdl"), None, None),
        P(("tok", "mdl"), None, None),
        P(("tok", "mdl"), None, None),
        P(("grp", "tok", "mdl"), None),
        P(("grp", "tok", "mdl"), None),
    )
    out_specs = (P(("grp", "tok", "mdl"), None), P(("grp", "tok"), "mdl", None, None))
    return jax.shard_map(shards, mesh=mesh, in_specs=in_specs, out_specs=out_specs, check_vma=False)
```

time: 214 us -> 157 us (0.73)
  matrix products: 48.7 us -> 26.6 us
  other arithmetic: 20 us -> 1.84 us
  Pallas kernels: 122 us -> 114 us
  local copies, waits for them, and re-layouts: 17.4 us -> 10.2 us
    dot_general x20 -> x0, matrix products: 22.3 us -> none  [the longest x8 12.1 us: second_pass(): jnp.dot(probs, block_values, preferred_element_type=jnp.float32)]
    lt x16 -> x0, other arithmetic: 10.6 us -> none  [block_scores(): allowed = row_offset + jnp.arange(block_len) < length]
    slice x3 -> x0, local copies, waits for them, and re-layouts: 5.63 us -> none  [the longest x1 3.91 us: shards(): cache[0, :, head_index, 1]]
    pallas_call x2 -> x3, Pallas kernels: 43 us -> 38.2 us  [the longest x2 36 us: collect(): pl.pallas_call(functools.partial(collect_kernel, groups, ranks, pieces),...]
    pallas_call x4, Pallas kernels: 79.4 us -> 75.9 us  [spread(): pl.pallas_call(functools.partial(spread_kernel, groups, ranks, cores, sam...]
    squeeze x2 -> x0, local copies, waits for them, and re-layouts: 2.23 us -> none  [shards(): cache[0, :, head_index, 1]]
    unnamed x52 -> x39, local copies, waits for them, and re-layouts: 3.42 us -> 4.86 us
where the time goes in v2:
time: 157 us
  Pallas kernels  114 us (73%)
  matrix products  26.6 us (17%)
  local copies, waits for them, and re-layouts  10.2 us (6%)
  blocking collectives  2.64 us (2%)
  other arithmetic  1.84 us (1%)
  between operations  1.72 us (1%)
    pallas_call x4, Pallas kernels, spread(): pl.pallas_call(functools.partial(spread_kernel, groups, ranks, cores, sam...  75.9 us
    pallas_call x2, Pallas kernels, collect(): pl.pallas_call(functools.partial(collect_kernel, groups, ranks, pieces),...  36 us
    dot_general x1, matrix products, shards(): up_val = jnp.dot(flat_rows, w_up[0], preferred_element_type=jnp.float32)  9.85 us
    dot_general x1, matrix products, shards(): gate_val = jnp.dot(flat_rows, w_gate[0], preferred_element_type=jnp.float32)  9.13 us
    unnamed x39, local copies, waits for them, and re-layouts  4.86 us
    dot_general x1, matrix products, shards(): jnp.dot(slab_hidden, w_down[0], preferred_element_type=jnp.float32)  4.82 us

profile of v2, /device:TPU:0, one launch (start us, length us, event | category | flops | bytes accessed | tf_op | source)
XLA Modules:
  0.0 157.1 jit_solution(15841421066906719680)
XLA Ops:
  0.6 0.0 copy-start
  0.6 0.0 copy-start.8
  0.7 2.6 %all_gather.3 = bf16[64,4096]{1,0:T(8,128)(2,1)S(1)} all-gather(bf16[64,2048]{1,0:T(8,128)(2,1)} %param.13), channel_id=1, replica_groups=mesh['grp'=2,'tok'=8,'mdl'=2] {'mdl'}, dimensions={1}, use_global_device_ids=true | all-gather | bytes 786432 | tf_op jit(solution)/shard_map/all_gather | solution.py:347
  3.3 0.2 fusion.17
  3.5 0.7 convert_element_type.61
  4.2 0.1 fusion.19
  4.4 14.0 %shard_map.140 = bf16[8,2,32,512]{3,2,1,0:T(8,128)(2,1)S(1)} custom-call(bf16[8,32,512]{2,1,0:T(8,128)(2,1)S(1)} %bitcast.74), custom_call_target="tpu_custom_call" | custom-call | tf_op jit(solution)/shard_map/pallas_call | solution.py:163
  18.4 0.0 copy-done.8
  18.4 0.2 reshape.120
  18.6 0.4 convolution_convert_fusion.1
  19.0 15.9 %shard_map.141 = bf16[8,64,512]{2,1,0:T(8,128)(2,1)S(1)} custom-call(bf16[8,64,512]{2,1,0:T(8,128)(2,1)S(1)} %bitcast.73), custom_call_target="tpu_custom_call" | custom-call | tf_op jit(solution)/shard_map/pallas_call | solution.py:163
  35.0 0.1 convert_reduce_fusion
  35.0 0.1 reshape.122
  35.9 0.2 multiply_cosine_fusion
  36.1 0.1 subtract_convert_fusion
  36.2 0.0 copy-start.9
  36.2 0.1 maximum_bitcast_fusion
  36.3 0.1 slice.20
  36.4 1.9 %copy.54 = bf16[1,2048,2,2,128]{4,1,3,2,0:T(8,128)(2,1)S(1)} copy(bf16[1,2048,2,2,128]{4,3,2,1,0:T(2,128)(2,1)} %param.15) | data formatting | bytes 4194304 | tf_op args[2]
  38.3 0.0 copy-done.9
  38.3 2.2 %shard_map.142.send = bf16[64,1024]{1,0:T(8,128)(2,1)S(1)} custom-call(s32[1]{0:T(128)} %copy.58.length, bf16[8,64,128]{2,1,0:T(8,128)(2,1)S(1)} %bitcast.77, bf16[2,2,2048,128]{3,2,1,0:T(8,128)(2,1)S(1)} %bitcast.71, bf16[2,2,64,128]{3,2,1,0:T(8,128)(2,1)S(1)} %get-tuple-element.11.fresh), custom_call_target="tpu_custom_call" | custom-call | tf_op jit(solution)/shard_map/pallas_call | solution.py:312
  40.5 18.1 %shard_map.143 = bf16[8,64,1024]{2,1,0:T(8,128)(2,1)S(1)} custom-call(bf16[64,1024]{1,0:T(8,128)(2,1)S(1)} %shard_map.142.send), custom_call_target="tpu_custom_call" | custom-call | tf_op jit(solution)/shard_map/pallas_call | solution.py:163
  58.6 0.7 convolution_convert_fusion.2
  59.3 0.0 copy-start.11
  59.3 0.0 copy-start.10
  59.3 10.4 %shard_map.144 = bf16[8,32,512]{2,1,0:T(8,128)(2,1)S(1)} custom-call(bf16[8,2,32,512]{3,2,1,0:T(8,128)(2,1)S(1)} %bitcast.76), custom_call_target="tpu_custom_call" | custom-call | tf_op jit(solution)/shard_map/pallas_call | solution.py:256
  69.7 0.1 convert_bitcast_fusion
  69.8 0.2 multiply_reduce_fusion
  70.1 0.1 copy.40
  70.2 0.1 reduce_window_sum.11
  70.2 0.1 copy.42
  70.3 0.0 copy-done.10
  70.3 0.3 copy-done.3
  70.6 0.4 convolution_convert_fusion.send
  71.0 27.9 %shard_map.145 = bf16[8,2,18,4096]{3,2,1,0:T(8,128)(2,1)S(1)} custom-call(bf16[4,18,4096]{2,1,0:T(8,128)(2,1)S(1)} %convolution_convert_fusion.send), custom_call_target="tpu_custom_call" | custom-call | tf_op jit(solution)/shard_map/pallas_call | solution.py:163
  99.0 2.3 %reshape.126 = bf16[288,4096]{1,0:T(8,128)(2,1)} reshape(bf16[8,2,18,4096]{3,2,1,0:T(8,128)(2,1)S(1)} %shard_map.145) | data formatting | bytes 4718592 | tf_op jit(solution)/shard_map/reshape | solution.py:399
  101.3 9.1 %fusion.4 = f32[288,1792]{1,0:T(8,128)S(1)} fusion(bf16[288,4096]{1,0:T(8,128)(2,1)} %reshape.126, bf16[1,4096,1792]{2,1,0:T(8,128)(2,1)} %param.21), kind=kOutput, calls=%fused_computation.4 | convolution fusion | flops 4227858432 | bytes 19103744 | tf_op jit(solution)/shard_map/dot_general | solution.py:400
  110.4 0.0 copy-done.7
  110.4 0.0 slice-start.2
  110.4 0.0 slice-start.3
  110.4 9.9 %fusion.14 = bf16[288,1792]{1,0:T(8,128)(2,1)S(1)} fusion(bf16[288,4096]{1,0:T(8,128)(2,1)S(1)} %copy-done.7, bf16[1,4096,1792]{2,1,0:T(8,128)(2,1)} %param.22, f32[288,1792]{1,0:T(8,128)S(1)} %fusion.4), kind=kOutput, calls=%fused_computation.12 | convolution fusion | flops 4230955008 | bytes 20135936 | tf_op jit(solution)/shard_map/dot_general | solution.py:401
  120.4 4.8 %fusion.6 = bf16[288,4096]{1,0:T(8,128)(2,1)S(1)} fusion(bf16[288,1792]{1,0:T(8,128)(2,1)S(1)} %fusion.14, bf16[1,1792,4096]{2,1,0:T(8,128)(2,1)S(1)} %bitcast.85), kind=kOutput, calls=%fused_computation.6 | convolution fusion | flops 4229038080 | bytes 18071552 | tf_op jit(solution)/shard_map/dot_general | solution.py:403
  125.2 0.0 copy-start.1
  125.2 2.4 %reshape.127.parts = bf16[8,2,18,4096]{3,2,1,0:T(8,128)(2,1)} reshape(bf16[288,4096]{1,0:T(8,128)(2,1)S(1)} %fusion.6) | data formatting | bytes 4718592 | tf_op jit(solution)/shard_map/reshape | solution.py:406
  127.6 1.9 %copy-done.2 = bf16[8,2,18,4096]{3,2,1,0:T(8,128)(2,1)S(1)} copy-done((bf16[8,2,18,4096]{3,2,1,0:T(8,128)(2,1)S(1)}, bf16[8,2,18,4096]{3,2,1,0:T(8,128)(2,1)}, u32[]{:S(2)}) %copy-start.2) | copy-done | bytes 2359320
  129.5 25.6 %shard_map.146 = bf16[4,18,4096]{2,1,0:T(8,128)(2,1)S(1)} custom-call(bf16[8,2,18,4096]{3,2,1,0:T(8,128)(2,1)S(1)} %copy-done.2), custom_call_target="tpu_custom_call" | custom-call | tf_op jit(solution)/shard_map/pallas_call | solution.py:256
  155.2 1.2 fusion.10
  156.4 0.7 copy.43
  (37 shorter events, 0.3 us)
Async XLA Ops:
  0.6 58.0 %copy-start = (bf16[8,128,512]{2,1,0:T(8,128)(2,1)S(1)}, bf16[8,128,512]{2,1,0:T(8,128)(2,1)}, u32[]{:S(2)}) copy-start(bf16[8,128,512]{2,1,0:T(8,128)(2,1)} %param.18) | copy-start | bytes 3145732
  0.6 17.7 %copy-start.8 = (bf16[512,2,2,128]{3,2,1,0:T(2,128)(2,1)S(1)}, bf16[512,2,2,128]{3,2,1,0:T(2,128)(2,1)}, u32[]{:S(2)}) copy-start(bf16[512,2,2,128]{3,2,1,0:T(2,128)(2,1)} %param.17) | copy-start | bytes 1572868
  3.3 67.0 %copy-start.5 = (bf16[64,4096]{1,0:T(8,128)(2,1)}, bf16[64,4096]{1,0:T(8,128)(2,1)S(1)}, u32[]{:S(2)}) copy-start(bf16[64,4096]{1,0:T(8,128)(2,1)S(1)} %all_gather.3) | copy-start | bytes 1572868
  36.2 2.1 %copy-start.9 = (bf16[64,8,128]{2,1,0:T(8,128)(2,1)S(1)}, bf16[64,8,128]{2,1,0:T(8,128)(2,1)}, u32[]{:S(2)}) copy-start(bf16[64,8,128]{2,1,0:T(8,128)(2,1)} %param.14) | copy-start | bytes 393220
  59.3 10.7 %copy-start.11 = (s32[32,2]{0,1:T(2,128)S(1)}, s32[32,2]{0,1:T(2,128)}, u32[]{:S(2)}) copy-start(s32[32,2]{0,1:T(2,128)} %param.24) | copy-start | bytes 772
  59.3 11.0 %copy-start.10 = (bf16[4096]{0:T(1024)(128)(2,1)S(1)}, bf16[4096]{0:T(1024)(128)(2,1)}, u32[]{:S(2)}) copy-start(bf16[4096]{0:T(1024)(128)(2,1)} %param.20) | copy-start | bytes 24580
  69.8 0.8 copy-start.3
  101.3 9.1 %copy-start.7 = (bf16[288,4096]{1,0:T(8,128)(2,1)S(1)}, bf16[288,4096]{1,0:T(8,128)(2,1)}, u32[]{:S(2)}) copy-start(bf16[288,4096]{1,0:T(8,128)(2,1)} %reshape.126) | copy-start | bytes 7077892
  101.3 19.0 %slice-start = ((s8[14680064]{0:T(1024)(128)(4,1)}), s8[4194304]{0:T(1024)(128)(4,1)S(1)}, s32[]{:S(2)}) async-start(s8[14680064]{0:T(1024)(128)(4,1)} %bitcast.84), calls=%async_computation | async-start | bytes 8388608
  101.3 19.0 %slice-start.1 = ((s8[14680064]{0:T(1024)(128)(4,1)}), s8[4194304]{0:T(1024)(128)(4,1)S(1)}, s32[]{:S(2)}) async-start(s8[14680064]{0:T(1024)(128)(4,1)} %bitcast.84), calls=%async_computation.1 | async-start | bytes 8388608
  110.4 9.9 %slice-start.2 = ((s8[14680064]{0:T(1024)(128)(4,1)}), s8[4194304]{0:T(1024)(128)(4,1)S(1)}, s32[]{:S(2)}) async-start(s8[14680064]{0:T(1024)(128)(4,1)} %bitcast.84), calls=%async_computation.2 | async-start | bytes 8388608
  110.4 9.9 %slice-start.3 = ((s8[14680064]{0:T(1024)(128)(4,1)}), s8[2097152]{0:T(1024)(128)(4,1)S(1)}, s32[]{:S(2)}) async-start(s8[14680064]{0:T(1024)(128)(4,1)} %bitcast.84), calls=%async_computation.3 | async-start | bytes 4194304
  125.2 31.9 %copy-start.1 = (bf16[8,128,512]{2,1,0:T(8,128)(2,1)S(1)}, bf16[8,128,512]{2,1,0:T(8,128)(2,1)}, u32[]{:S(2)}) copy-start(bf16[8,128,512]{2,1,0:T(8,128)(2,1)} %param.18) | copy-start | bytes 3145732
  127.6 1.9 %copy-start.2 = (bf16[8,2,18,4096]{3,2,1,0:T(8,128)(2,1)S(1)}, bf16[8,2,18,4096]{3,2,1,0:T(8,128)(2,1)}, u32[]{:S(2)}) copy-start(bf16[8,2,18,4096]{3,2,1,0:T(8,128)(2,1)} %reshape.127.parts) | copy-start | bytes 7077892
  129.5 25.6 %copy-start.12 = (f32[32,2]{0,1:T(2,128)S(1)}, f32[32,2]{0,1:T(2,128)}, u32[]{:S(2)}) copy-start(f32[32,2]{0,1:T(2,128)} %param.25) | copy-start | bytes 772
  129.5 25.7 %copy-start.4 = (f32[8,4,8,512]{3,2,0,1:T(8,128)S(1)}, f32[8,4,8,512]{3,2,0,1:T(8,128)}, u32[]{:S(2)}) copy-start(f32[8,4,8,512]{3,2,0,1:T(8,128)} %copy-done.3) | copy-start | bytes 1572868
  129.5 25.7 %copy-start.6 = (bf16[64,4096]{1,0:T(8,128)(2,1)S(1)}, bf16[64,4096]{1,0:T(8,128)(2,1)}, u32[]{:S(2)}) copy-start(bf16[64,4096]{1,0:T(8,128)(2,1)} %copy-done.5) | copy-start | bytes 1572868
